TPU v7x, 32 devices: a 4x4x1 block of a 4x4x8 slice. The times are simulated.
32 devices in a mesh: data: 1 (over z), tp: 4 (over y), ep: 8 (over x, core).
Axes of the slice: x: 4, y: 4, z: 1, core: 2. Of those that a mesh axis runs over, the one named last changes fastest.
The devices are a block of a 4x4x8 slice.
Arguments:
- tokens: bfloat16 [4096, 2560], P(('data', 'ep', 'tp'))
- expert_ids: int32 [4096, 6], P(('data', 'ep', 'tp'))
- gate_vals: float32 [4096, 6], P(('data', 'ep', 'tp'))
- slot_ids: int32 [4096, 6], P(('data', 'ep', 'tp'))
- send_counts: int32 [32, 64], P(('data', 'ep', 'tp'))
- shared_w1: bfloat16 [2560, 3072], P(None, 'tp')
- shared_w3: bfloat16 [2560, 3072], P(None, 'tp')
- shared_w2: bfloat16 [3072, 2560], P('tp')
- expert_w1: bfloat16 [64, 2560, 1536], P('ep')
- expert_w3: bfloat16 [64, 2560, 1536], P('ep')
- expert_w2: bfloat16 [64, 1536, 2560], P('ep')
Outputs:
- output: bfloat16 [4096, 2560], P(('data', 'ep', 'tp'))
All inputs are finite; a program needn't handle non-finite values.
Results may differ from a plain program's by a relative error of at most 0.001.
Values are sent between devices in bfloat16 or wider.
A program may use at most 768 MiB of HBM per device.

v0:
```python
import jax
import jax.numpy as jnp
from jax import lax
from jax.sharding import PartitionSpec as P

CAP_FACTOR = 4


def capacity_rows(n_tok, top_k, n_exp):
    return min(n_tok, ((CAP_FACTOR * n_tok * top_k // n_exp + 7) // 8) * 8)


def solution(mesh):
    ep_size = mesh.shape["ep"]
    row_spec = P(("data", "ep", "tp"), None)
    expert_spec = P("ep", None, None)

    def layer_body(tokens, expert_ids, gate_vals, slot_ids, send_counts, shared_w1, shared_w3, shared_w2, expert_w1, expert_w3, expert_w2):
        n_tok, d_model = tokens.shape
        top_k = expert_ids.shape[1]
        n_local = expert_w1.shape[0]
        n_exp = n_local * ep_size
        capacity = capacity_rows(n_tok, top_k, n_exp)
        n_rows = n_exp * capacity

        gathered = lax.all_gather(tokens, "tp", axis=0, tiled=True)
        pre_gate = jnp.dot(gathered, shared_w1, preferred_element_type=jnp.float32)
        pre_up = jnp.dot(gathered, shared_w3, preferred_element_type=jnp.float32)
        shared_hidden = (jax.nn.silu(pre_gate) * pre_up).astype(jnp.bfloat16)
        part_sum = jnp.dot(shared_hidden, shared_w2, preferred_element_type=jnp.float32)
        shared_out = lax.psum_scatter(part_sum, "tp", scatter_dimension=0, tiled=True)

        row_limit = jnp.take(send_counts[0], expert_ids, axis=0)
        kept_mask = (slot_ids >= 0) & (slot_ids < row_limit)
        dest_row = jnp.where(kept_mask, expert_ids * capacity + slot_ids, n_rows)
        tok_ids = jnp.broadcast_to(jnp.arange(n_tok, dtype=jnp.int32)[:, None], (n_tok, top_k)).reshape(-1)
        owner_ids = jnp.full((n_rows,), n_tok, jnp.int32).at[dest_row.reshape(-1)].set(tok_ids, mode="drop")
        send_buf = jnp.take(tokens, owner_ids, axis=0, mode="fill", fill_value=0)
        send_buf = send_buf.reshape(ep_size, n_local, capacity, d_model)
        recv_buf = lax.all_to_all(send_buf, "ep", 0, 2, tiled=True)
        recv_buf = recv_buf.reshape(n_local, ep_size * capacity, d_model)

        exp_gate = jnp.einsum("erd,edf->erf", recv_buf, expert_w1, preferred_element_type=jnp.float32)
        exp_up = jnp.einsum("erd,edf->erf", recv_buf, expert_w3, preferred_element_type=jnp.float32)
        exp_hidden = (jax.nn.silu(exp_gate) * exp_up).astype(jnp.bfloat16)
        exp_out = jnp.einsum("erf,efd->erd", exp_hidden, expert_w2, preferred_element_type=jnp.float32).astype(jnp.bfloat16)
        back_buf = lax.all_to_all(exp_out.reshape(1, n_local, ep_size * capacity, d_model), "ep", 2, 0, tiled=True)

        back_rows = back_buf.reshape(n_rows, d_model)
        picked = jnp.take(back_rows, dest_row, axis=0, mode="fill", fill_value=0)
        gate_eff = jnp.where(kept_mask, gate_vals, 0.0)
        routed_sum = jnp.sum(gate_eff[:, :, None] * picked.astype(jnp.float32), axis=1)
        return (tokens.astype(jnp.float32) + shared_out + routed_sum).astype(jnp.bfloat16)

    return jax.shard_map(
        layer_body,
        mesh=mesh,
        in_specs=(row_spec, row_spec, row_spec, row_spec, row_spec, P(None, "tp"), P(None, "tp"), P("tp", None), expert_spec, expert_spec, expert_spec),
        out_specs=row_spec,
        check_vma=False,
    )
```

profile of v0, /device:TPU:97, one launch (start us, length us, event | category | flops | bytes accessed | tf_op | source)
XLA Modules:
  0.0 611.9 jit_solution(6445886739007995267)
XLA Ops:
  6.5 0.0 copy-start
  6.6 0.7 compare_select_fusion.3
  7.3 0.1 copy.46
  7.4 0.1 reshape.75
  7.5 0.0 copy-done
  7.5 0.0 copy-start.6
  7.5 0.0 copy-start.10
  7.6 0.0 copy-start.2
  7.6 4.8 gather_fusion
  12.4 0.1 reshape.74
  12.5 0.1 copy.47
  12.6 0.0 copy-done.6
  12.6 0.0 copy-done.10
  12.6 0.6 compare_and_fusion.1
  13.1 0.0 copy-start.4
  13.1 0.1 copy.50
  13.3 0.1 reshape.68
  13.4 0.1 reshape.101
  13.6 3.4 scatter_custom_fusion
  17.0 0.1 broadcast_in_dim.60
  17.1 0.0 copy-done.2
  17.1 16.8 %gather_fusion.1 = bf16[3072,2560]{1,0:T(8,128)(2,1)} fusion(bf16[128,2560]{1,0:T(8,128)(2,1)S(1)} %copy-done.2, s32[3072]{0:T(1024)S(1)} %fusion.1), kind=kCustom, calls=%fused_computation.1 | custom fusion | bytes 31469568 | tf_op jit(solution)/shard_map/jit(_take)/gather | solution.py:38
  34.0 0.0 copy-done.4
  34.0 13.5 %broadcast_select_fusion = bf16[8,8,48,2560]{3,2,1,0:T(8,128)(2,1)} fusion(bf16[8,8,48,2560]{3,2,1,0:T(8,128)(2,1)} %bitcast.43, pred[8,8,48]{2,1,0:T(8,128)(4,1)S(1)} %broadcast_in_dim.60), kind=kLoop, calls=%fused_computation.6 | loop fusion | flops 7864320 | bytes 31460352 | tf_op jit(solution)/shard_map/jit(_take)/select_n | solution.py:38
  47.4 7.6 %all-to-all-start = ((bf16[8,8,48,2560]{3,2,1,0:T(8,128)(2,1)}), bf16[8,8,48,2560]{3,2,1,0:T(8,128)(2,1)}, u32[]{:S(2)}, u32[]{:S(2)}) async-start(bf16[8,8,48,2560]{3,2,1,0:T(8,128)(2,1)} %broadcast_select_fusion), calls=%async_computation.1 | async-start | bytes 31457280 | tf_op jit(solution)/shard_map/all_to_all | solution.py:40
  55.0 0.0 all-gather.2.cloned.1.call-start
  55.0 0.7 all-gather.2.cloned.1.call-update
  55.8 171.5 %all-to-all-done = bf16[8,8,48,2560]{3,2,1,0:T(8,128)(2,1)} async-done(((bf16[8,8,48,2560]{3,2,1,0:T(8,128)(2,1)}), bf16[8,8,48,2560]{3,2,1,0:T(8,128)(2,1)}, u32[]{:S(2)}, u32[]{:S(2)}) %all-to-all-start) | async-done | bytes 15728672 | tf_op jit(solution)/shard_map/all_to_all | solution.py:40
  227.2 13.1 %copy.51 = bf16[1,8,8,48,2560]{4,3,2,1,0:T(8,128)(2,1)} copy(bf16[1,8,8,48,2560]{4,3,1,2,0:T(8,128)(2,1)} %bitcast.3) | data formatting | bytes 31457280 | tf_op jit(solution)/shard_map/all_to_all | solution.py:40
  240.4 40.2 %fusion.9 = f32[8,384,1536]{2,1,0:T(8,128)} fusion(bf16[8,384,2560]{2,1,0:T(8,128)(2,1)} %bitcast.40, bf16[8,2560,1536]{2,1,0:T(8,128)(2,1)} %param.19), kind=kOutput, calls=%fused_computation.29 | convolution fusion | flops 24159191040 | bytes 97517568 | tf_op jit(solution)/shard_map/erd,edf->erf/dot_general | solution.py:43
  280.6 62.5 %convert_bitcast_fusion = bf16[1,8,384,2560]{3,2,1,0:T(8,128)(2,1)} fusion(bf16[8,1536,2560]{2,1,0:T(8,128)(2,1)} %param.21, f32[8,384,1536]{2,1,0:T(8,128)} %fusion.9, bf16[8,384,2560]{2,1,0:T(8,128)(2,1)} %bitcast.41, bf16[8,2560,1536]{2,1,0:T(8,128)(2,1)} %param.20), kind=kOutput, calls=%fused_computation.5 | convolution fusion | flops 48354557952 | bytes 176160768 | tf_op jit(solution)/shard_map/erf,efd->erd/dot_general | solution.py:46
  343.1 32.5 %copy.52 = bf16[1,8,384,2560]{3,1,0,2:T(8,128)(2,1)} copy(bf16[1,8,384,2560]{3,2,1,0:T(8,128)(2,1)} %convert_bitcast_fusion) | data formatting | bytes 31457280 | tf_op jit(solution)/shard_map/reshape | solution.py:47
  375.6 6.8 %all-to-all-start.1 = ((bf16[1,8,384,2560]{3,1,0,2:T(8,128)(2,1)}), bf16[1,8,384,2560]{3,1,0,2:T(8,128)(2,1)}, u32[]{:S(2)}, u32[]{:S(2)}) async-start(bf16[1,8,384,2560]{3,1,0,2:T(8,128)(2,1)} %copy.52), calls=%async_computation.2 | async-start | bytes 31457280 | tf_op jit(solution)/shard_map/all_to_all | solution.py:47
  382.4 0.0 reduce-scatter.2.cloned.1.call-start
  382.4 0.0 all-gather.2.cloned.1.call-done
  382.4 0.0 copy-start.11
  382.5 6.4 %fusion.8 = f32[512,768]{1,0:T(8,128)} fusion(bf16[512,2560]{1,0:T(8,128)(2,1)} %all-gather.2.cloned.1.call-done, bf16[2560,768]{1,0:T(8,128)(2,1)} %param.16), kind=kOutput, calls=%fused_computation.28 | convolution fusion | flops 2013265920 | bytes 8126464 | tf_op jit(solution)/shard_map/dot_general | solution.py:27
  388.9 0.0 copy-done.11
  388.9 0.0 copy-start.5
  388.9 0.0 copy-start.8
  388.9 0.0 copy-start.9
  388.9 0.0 copy-start.7
  388.9 11.7 %fusion = f32[512,2560]{1,0:T(8,128)} fusion(bf16[768,2560]{1,0:T(8,128)(2,1)} %param.18, f32[512,768]{1,0:T(8,128)} %fusion.8, bf16[512,2560]{1,0:T(8,128)(2,1)S(1)} %copy-done.11, bf16[2560,768]{1,0:T(8,128)(2,1)} %param.17), kind=kOutput, calls=%fused_computation.10 | convolution fusion | flops 4028891136 | bytes 17301504 | tf_op jit(solution)/shard_map/dot_general | solution.py:30
  400.6 0.1 reduce-scatter.2.cloned.1.call-update
  400.6 0.0 copy-done.5
  400.6 0.1 copy.54
  400.8 0.1 reshape.91
  400.9 0.0 copy-done.8
  400.9 0.0 copy-done.9
  400.9 0.1 copy.48
  401.0 0.0 copy-done.7
  401.0 0.1 copy.49
  401.2 153.5 %all-to-all-done.1 = bf16[1,8,384,2560]{3,1,0,2:T(8,128)(2,1)} async-done(((bf16[1,8,384,2560]{3,1,0,2:T(8,128)(2,1)}), bf16[1,8,384,2560]{3,1,0,2:T(8,128)(2,1)}, u32[]{:S(2)}, u32[]{:S(2)}) %all-to-all-start.1) | async-done | bytes 15728672 | tf_op jit(solution)/shard_map/all_to_all | solution.py:47
  554.7 16.6 %copy.53 = bf16[1,8,8,48,2560]{4,3,1,2,0:T(8,128)(2,1)} copy(bf16[1,8,8,48,2560]{4,1,3,2,0:T(8,128)(2,1)} %bitcast.6) | data formatting | bytes 31457280 | tf_op jit(solution)/shard_map/all_to_all | solution.py:47
  571.3 0.0 copy-start.1
  571.3 15.9 %gather_fusion.2 = bf16[768,2560]{1,0:T(8,128)(2,1)} fusion(bf16[3072,2560]{1,0:T(8,128)(2,1)} %bitcast.42, s32[1024]{0:T(1024)S(1)} %pad_clamp_fusion), kind=kCustom, calls=%fused_computation.2 | custom fusion | bytes 7867392 | tf_op jit(solution)/shard_map/jit(_take)/gather | solution.py:50
  587.2 0.0 copy-start.3
  587.2 7.2 %reshape.90 = bf16[128,6,2560]{2,1,0:T(8,128)(2,1)} reshape(bf16[768,2560]{1,0:T(8,128)(2,1)} %gather_fusion.2) | data formatting | bytes 7864320 | tf_op jit(solution)/shard_map/jit(_take)/gather | solution.py:50
  594.4 8.2 %multiply_reduce_fusion = f32[128,2560]{1,0:T(8,128)S(1)} fusion(bf16[128,6,2560]{2,1,0:T(8,128)(2,1)} %reshape.90, f32[128,6]{1,0:T(8,128)S(1)} %copy.48, pred[128,6]{1,0:T(8,128)(4,1)S(1)} %copy.49), kind=kLoop, calls=%fused_computation.7 | loop fusion | flops 7536640 | bytes 5246720 | tf_op jit(solution)/shard_map/reduce_sum | solution.py:52
  602.6 0.0 reduce-scatter.2.cloned.1.call-done
  602.6 0.0 copy-done.3
  602.7 2.4 add_convert_fusion
  605.1 0.0 copy-done.1
  (8 shorter events, 0.1 us)
Async XLA Ops:
  6.5 1.0 copy-start
  7.5 5.0 copy-start.6
  7.5 5.0 copy-start.10
  7.6 9.5 %copy-start.2 = (bf16[128,2560]{1,0:T(8,128)(2,1)S(1)}, bf16[128,2560]{1,0:T(8,128)(2,1)}, u32[]{:S(2)}) copy-start(bf16[128,2560]{1,0:T(8,128)(2,1)} %param.11) | copy-start | bytes 1966084
  13.1 20.8 %copy-start.4 = (s32[128,6]{0,1:T(8,128)}, s32[128,6]{0,1:T(8,128)S(1)}, u32[]{:S(2)}) copy-start(s32[128,6]{0,1:T(8,128)S(1)} %get-tuple-element.6) | copy-start | bytes 9220
  47.4 179.8 %all-to-all-start = ((bf16[8,8,48,2560]{3,2,1,0:T(8,128)(2,1)}), bf16[8,8,48,2560]{3,2,1,0:T(8,128)(2,1)}, u32[]{:S(2)}, u32[]{:S(2)}) async-start(bf16[8,8,48,2560]{3,2,1,0:T(8,128)(2,1)} %broadcast_select_fusion), calls=%async_computation.1 | async-start | bytes 31457280 | tf_op jit(solution)/shard_map/all_to_all | solution.py:40
  55.0 327.5 %all-gather.2.cloned.1.call-start = ((), (), s32[]{:S(2)}) async-start(), calls=%async_computation.3 | async-start | bytes 3276800 | tf_op jit(solution)/shard_map/all_gather | solution.py:26
  375.6 179.1 %all-to-all-start.1 = ((bf16[1,8,384,2560]{3,1,0,2:T(8,128)(2,1)}), bf16[1,8,384,2560]{3,1,0,2:T(8,128)(2,1)}, u32[]{:S(2)}, u32[]{:S(2)}) async-start(bf16[1,8,384,2560]{3,1,0,2:T(8,128)(2,1)} %copy.52), calls=%async_computation.2 | async-start | bytes 31457280 | tf_op jit(solution)/shard_map/all_to_all | solution.py:47
  382.4 220.2 %reduce-scatter.2.cloned.1.call-start = ((), (), s32[]{:S(2)}) async-start(), calls=%async_computation.4 | async-start | bytes 6553600 | tf_op jit(solution)/shard_map/reduce_scatter | solution.py:31
  382.4 6.4 %copy-start.11 = (bf16[512,2560]{1,0:T(8,128)(2,1)S(1)}, bf16[512,2560]{1,0:T(8,128)(2,1)}, u32[]{:S(2)}) copy-start(bf16[512,2560]{1,0:T(8,128)(2,1)} %all-gather.2.cloned.1.call-done) | copy-start | bytes 7864324
  388.9 11.7 %copy-start.5 = (s32[128,6]{0,1:T(8,128)S(1)}, s32[128,6]{0,1:T(8,128)}, u32[]{:S(2)}) copy-start(s32[128,6]{0,1:T(8,128)} %copy-done.4) | copy-start | bytes 9220
  388.9 12.0 %copy-start.8 = (pred[128,6]{0,1:T(8,128)(4,1)S(1)}, pred[128,6]{0,1:T(8,128)(4,1)}, u32[]{:S(2)}) copy-start(pred[128,6]{0,1:T(8,128)(4,1)} %get-tuple-element.7) | copy-start | bytes 2308
  388.9 12.0 %copy-start.9 = (f32[128,6]{0,1:T(8,128)S(1)}, f32[128,6]{0,1:T(8,128)}, u32[]{:S(2)}) copy-start(f32[128,6]{0,1:T(8,128)} %param.13) | copy-start | bytes 9220
  388.9 12.2 %copy-start.7 = (pred[128,6]{0,1:T(8,128)(4,1)S(1)}, pred[128,6]{0,1:T(8,128)(4,1)}, u32[]{:S(2)}) copy-start(pred[128,6]{0,1:T(8,128)(4,1)} %get-tuple-element.5) | copy-start | bytes 2308
  571.3 33.8 %copy-start.1 = (s32[1,64]{1,0:T(1,128)S(1)}, s32[1,64]{1,0:T(1,128)}, u32[]{:S(2)}) copy-start(s32[1,64]{1,0:T(1,128)} %param.15) | copy-start | bytes 772
  587.2 15.4 %copy-start.3 = (bf16[128,2560]{1,0:T(8,128)(2,1)S(1)}, bf16[128,2560]{1,0:T(8,128)(2,1)}, u32[]{:S(2)}) copy-start(bf16[128,2560]{1,0:T(8,128)(2,1)} %param.11) | copy-start | bytes 1966084
Sparse Core Ops, SparseCore 0:
  57.4 34.2 all-gather.1
  400.7 54.8 reduce-scatter.1
where the time goes:
time: 613 us; the launch traced here: 612 us
  waiting for transfers between devices  326 us (53%)
  matrix products  121 us (20%)
  local copies, waits for them, and re-layouts  112 us (18%)
  other arithmetic  25.5 us (4%)
  starting transfers between devices  14.4 us (2%)
  between operations  13.6 us (2%)
    all_to_all x1, waiting for transfers between devices, layer_body(): recv_buf = lax.all_to_all(send_buf, 'ep', 0, 2, tiled=True)  171 us
    all_to_all x1, waiting for transfers between devices, layer_body(): lax.all_to_all(exp_out.reshape(1, n_local, ep_size * capacity, d_model),...  153 us
    dot_general x1, matrix products, layer_body(): jnp.einsum('erf,efd->erd', exp_hidden, expert_w2, preferred_element_type=...  62.5 us
    dot_general x1, matrix products, layer_body(): jnp.einsum('erd,edf->erf', recv_buf, expert_w1, preferred_element_type=jn...  40.2 us
    reshape x1, local copies, waits for them, and re-layouts, layer_body(): exp_out.reshape(1, n_local, ep_size * capacity, d_model)  32.5 us
    gather x2, local copies, waits for them, and re-layouts, layer_body(): picked = jnp.take(back_rows, dest_row, axis=0, mode='fill', fill_value=0)  23.1 us
    gather x1, local copies, waits for them, and re-layouts, layer_body(): send_buf = jnp.take(tokens, owner_ids, axis=0, mode='fill', fill_value=0)  16.8 us
    all_to_all x1, local copies, waits for them, and re-layouts, layer_body(): lax.all_to_all(exp_out.reshape(1, n_local, ep_size * capacity, d_model),...  16.6 us
  transfers between devices with their start and end apart: 4, of which 2 were waited for; matrix products, arithmetic and copies ran while one was open for 35% of the time, Pallas kernels for 0%

commit v1 on v0

v1 whole, which is shorter than its diff:
```python
import functools

import jax
import jax.numpy as jnp
from jax import lax
from jax.experimental import pallas as pl
from jax.experimental.pallas import tpu as pltpu
from jax.sharding import PartitionSpec as P

CAP_FACTOR = 4
BF = jnp.bfloat16
F32 = jnp.float32
MESH = pl.DeviceIdType.MESH
BLK = 256
META = 16


def capacity_rows(n_tok, top_k, n_exp):
    return min(n_tok, ((CAP_FACTOR * n_tok * top_k // n_exp + 7) // 8) * 8)


def silu_mul(g, u):
    return (g * (1.0 / (1.0 + jnp.exp(-g))) * u).astype(BF)


def dot(a, b):
    return jnp.dot(a, b, preferred_element_type=F32)


def layer_kernel(cfg, tok, meta, ws1, ws3, ws2, w1, w3, w2, out,
                 hr, xg, mg, pb, sb, d2d, far, fin, yfar, yfin, acc, sh, gu, gm, ring,
                 own_sem, xs, xr, ps, pr, ms, mr, ys, yr, wsem,
                 ysend, yrecv, dsend, drecv, fsend, frecv, nsend, nrecv):
    EP, TP, NT, D, FF, FS, NL, CAP, TOPK, NS = cfg
    ROWS = EP * CAP
    LROWS = NL * CAP
    H = NT // 2
    NX = EP // 2
    NB = D // BLK
    C1 = FF // BLK
    Q1 = NL * C1
    PAIRS = NL // 2
    Q2 = NB * PAIRS
    SA = FS // BLK
    SB = D // (2 * BLK)

    me = lax.axis_index("ep")
    ty = lax.axis_index("tp")
    cx = me // 2
    cc = me % 2
    mate = cx * 2 + (1 - cc)
    rx = (cx + 1) % NX
    lx = (cx + NX - 1) % NX
    fx = (cx + 2) % NX
    right = {"ep": rx * 2 + cc}
    left = {"ep": lx * 2 + cc}
    up = {"tp": (ty + 1) % TP}
    down = {"tp": (ty + TP - 1) % TP}
    partner = {"ep": mate}

    def remote(src, dst, ssem, rsem, dev):
        return pltpu.make_async_remote_copy(src_ref=src, dst_ref=dst, send_sem=ssem, recv_sem=rsem, device_id=dev, device_id_type=MESH)

    def wpair(slot, ra, rb, n):
        return (pltpu.make_async_copy(ra, ring.at[slot, pl.ds(0, n), pl.ds(0, BLK)], wsem.at[slot, 0]),
                pltpu.make_async_copy(rb, ring.at[slot, pl.ds(0, n), pl.ds(BLK, BLK)], wsem.at[slot, 1]))

    def cols(i, w=BLK):
        return pl.ds(pl.multiple_of(i * w, w), w)

    def chunk_a(i):
        return wpair(i % NS, ws1.at[:, cols(i)], ws3.at[:, cols(i)], D)

    def chunk_b(i):
        return wpair((i + SA) % NS, ws2.at[:, cols(2 * i)], ws2.at[:, cols(2 * i + 1)], FS)

    def chunk_1(q):
        e, n = q // C1, q % C1
        return wpair((q + SA + SB) % NS, w1.at[e, :, cols(n)], w3.at[e, :, cols(n)], D)

    def chunk_2(q):
        b, p = q // PAIRS, q % PAIRS
        return wpair((q + SA + SB + Q1) % NS, w2.at[2 * p, :, cols(b)], w2.at[2 * p + 1, :, cols(b)], FF)

    def start(pair):
        pair[0].start()
        pair[1].start()

    def wait(pair):
        pair[0].wait()
        pair[1].wait()

    total = SA + SB + Q1 + Q2

    def start_at(i):
        bounds = ((0, SA, chunk_a), (SA, SA + SB, chunk_b), (SA + SB, SA + SB + Q1, chunk_1), (SA + SB + Q1, total, chunk_2))
        for lo, hi, fn in bounds:
            if isinstance(i, int):
                if lo <= i < hi:
                    start(fn(i - lo))
            else:
                @pl.when((i >= lo) & (i < hi))
                def _(fn=fn, lo=lo):
                    start(fn(i - lo))

    own = pltpu.make_async_copy(tok, xg.at[me], own_sem)
    own.start()
    for i in range(NS - 1):
        start_at(i)

    barrier = pltpu.get_barrier_semaphore()
    for d in range(1, EP):
        pl.semaphore_signal(barrier, inc=1, device_id={"ep": (me + d) % EP}, device_id_type=MESH)
    for dev in (up, down):
        pl.semaphore_signal(barrier, inc=1, device_id=dev, device_id_type=MESH)
    mg[me] = meta[...]
    own.wait()
    pl.semaphore_wait(barrier, EP + 1)

    lo_h, hi_h, all_h = pl.ds(0, H), pl.ds(H, H), pl.ds(0, NT)

    def xpart(dx, part):
        return xg.at[((cx + dx + NX) % NX) * 2 + cc, part, :]

    def xsend(k, dx, part, dev):
        ref = xpart(dx, part)
        return remote(ref, ref, xs.at[k], xr.at[k], dev)

    x_r0 = xsend(0, 0, lo_h, right)
    x_r1 = xsend(1, 0, hi_h, right)
    x_l1 = xsend(2, 0, hi_h, left)
    x_l0 = xsend(3, 0, lo_h, left)
    x_fr = xsend(4, -1, lo_h, right)
    x_fl = xsend(5, 1, hi_h, left)

    def psend(k, dx, part):
        ref = xpart(dx, part)
        return remote(ref, ref, ps.at[k], pr.at[k], partner)

    p_own = psend(0, 0, all_h)
    p_l = psend(1, -1, all_h)
    p_r = psend(2, 1, all_h)
    p_f0 = psend(3, 2, lo_h)
    p_f1 = psend(4, 2, hi_h)

    def ypart(j, part_start, n):
        return hr.at[0, pl.ds(j * NT + part_start, n), :]

    y_r0 = remote(xg.at[me, lo_h, :], ypart(0, 0, H), ys.at[0], yr.at[0], up)
    y_r1 = remote(xg.at[me, hi_h, :], ypart(0, H, H), ys.at[1], yr.at[1], up)
    y_l1 = remote(xg.at[me, hi_h, :], ypart(1, H, H), ys.at[2], yr.at[2], down)
    y_l0 = remote(xg.at[me, lo_h, :], ypart(1, 0, H), ys.at[3], yr.at[3], down)
    y_fr = remote(ypart(0, 0, H), ypart(2, 0, H), ys.at[4], yr.at[4], up)
    y_fl = remote(ypart(1, H, H), ypart(2, H, H), ys.at[5], yr.at[5], down)

    metas = [remote(mg.at[me], mg.at[me], ms.at[d - 1], mr.at[d - 1], {"ep": (me + d) % EP}) for d in range(1, EP)]

    for c in metas:
        c.start()
    for c in (x_r0, x_l1, y_r0, y_l1, p_own, x_r1, x_l0, y_r1, y_l0):
        c.start()

    row_id = lax.broadcasted_iota(jnp.int32, (LROWS, NT), 0).astype(F32) + (me * LROWS).astype(F32)

    def gather(k, _):
        k2 = k // 2
        dx = (3 * k2 + 3 * (k2 // 2) - 2 * (k2 // 3)) % NX
        s = ((cx + dx) % NX) * 2 + (cc + k) % 2
        m = mg[s]
        pick = jnp.zeros((LROWS, NT), F32)
        wgt = jnp.zeros((LROWS, NT), F32)
        for j in range(TOPK):
            hit = m[j:j + 1, :] == row_id
            pick = jnp.where(hit, 1.0, pick)
            wgt = wgt + jnp.where(hit, m[8 + j:9 + j, :], 0.0)
        pick = pick.astype(BF)
        wt = jnp.transpose(wgt)
        hi = wt.astype(BF)
        rest = wt - hi.astype(F32)
        mid = rest.astype(BF)
        low = (rest - mid.astype(F32)).astype(BF)
        gm[s, 0:NT, :] = hi
        gm[s, NT:2 * NT, :] = mid
        gm[s, 2 * NT:3 * NT, :] = low
        place = pl.ds(pl.multiple_of(s * CAP, CAP), CAP)
        for n in range(D // 512):
            part = slice(n * 512, (n + 1) * 512)
            got = dot(pick, xg[s, :, part]).astype(BF)
            for e in range(NL):
                hr[e + 1, place, part] = got[e * CAP:(e + 1) * CAP, :]
        return 0

    for c in metas:
        c.wait_recv()
    lax.fori_loop(0, 1, gather, 0)

    x_r0.wait_recv()
    x_fr.start()
    x_l1.wait_recv()
    x_fl.start()
    y_r0.wait_recv()
    y_fr.start()
    y_l1.wait_recv()
    y_fl.start()
    x_r1.wait_recv()
    p_l.start()
    x_l0.wait_recv()
    p_r.start()
    y_r1.wait_recv()
    y_l0.wait_recv()
    p_own.wait_recv()
    p_l.wait_recv()
    p_r.wait_recv()
    lax.fori_loop(1, 6, gather, 0)
    x_fr.wait_recv()
    p_f0.start()
    x_fl.wait_recv()
    p_f1.start()
    y_fr.wait_recv()
    y_fl.wait_recv()

    def shared_in(n, _):
        wait(chunk_a(n))
        slot = n % NS
        start_at(n - 1 + NS)
        a = dot(hr[0], ring[slot])
        b = dot(xg[me], ring[slot])
        sh[pl.ds(NT, 3 * NT), cols(n)] = silu_mul(a[:, :BLK], a[:, BLK:])
        sh[pl.ds(0, NT), cols(n)] = silu_mul(b[:, :BLK], b[:, BLK:])
        return 0

    lax.fori_loop(0, SA, shared_in, 0)

    def shared_out(i, _):
        wait(chunk_b(i))
        slot = (i + SA) % NS
        start_at(i + SA - 1 + NS)
        r = dot(sh[...], ring[slot, pl.ds(0, FS), :])
        here = pl.ds(pl.multiple_of(i * 2 * BLK, 2 * BLK), 2 * BLK)
        acc[:, here] = xg[me, :, here].astype(F32) + r[0:NT, :]
        for j in range(3):
            for h in range(2):
                pb[2 * i + h, j] = r[(j + 1) * NT:(j + 2) * NT, h * BLK:(h + 1) * BLK]
        return 0

    lax.fori_loop(0, SB, shared_out, 0)

    def y_half(k, dev):
        return remote(pb.at[:, 2, pl.ds(k * H, H), :], yfar.at[k], ysend.at[k], yrecv.at[k], dev)

    def y_full(k, j, dev):
        return remote(pb.at[:, j], yfin.at[k], ysend.at[2 + k], yrecv.at[2 + k], dev)

    y_halves = (y_half(0, up), y_half(1, down))
    y_fulls = (y_full(0, 1, up), y_full(1, 0, down))
    for c in y_halves:
        c.start()

    p_f0.wait_recv()
    p_f1.wait_recv()
    lax.fori_loop(6, EP, gather, 0)

    def y_step2():
        for c in y_halves:
            c.wait()

        def add(i, _):
            pb[i, 1, 0:H, :] += yfar[0, i]
            pb[i, 0, H:NT, :] += yfar[1, i]
            return 0

        lax.fori_loop(0, NB, add, 0)
        for c in y_fulls:
            c.start()

    def y_step3():
        for c in y_fulls:
            c.wait()

        def add(i, _):
            acc[:, cols(i)] += yfin[0, i] + yfin[1, i]
            return 0

        lax.fori_loop(0, NB, add, 0)

    y_fr.wait_send()
    y_fl.wait_send()

    def finish(e, n):
        g = gu[n % 2]
        hr[e, :, n * BLK:(n + 1) * BLK] = silu_mul(g[:, :BLK], g[:, BLK:])

    def first(e, _):
        @pl.when(e == 2)
        def _():
            y_step2()

        @pl.when(e == NL - 1)
        def _():
            y_step3()

        for n in range(C1):
            q = e * C1 + n
            wait(chunk_1(q))
            start_at(SA + SB + q - 1 + NS)
            gu[n % 2] = dot(hr[e + 1], ring[(q + SA + SB) % NS])
            if n:
                finish(e, n - 1)
            else:
                finish(jnp.maximum(e - 1, 0), C1 - 1)
        return 0

    lax.fori_loop(0, NL, first, 0)
    finish(NL - 1, C1 - 1)

    def to_mate(b):
        return remote(sb.at[b % 2], d2d.at[b], dsend.at[b], drecv.at[b], partner)

    def half(b, k, dev):
        return remote(pb.at[b, fx, pl.ds(k * H, H), :], far.at[k, b], fsend.at[k, b], frecv.at[k, b], dev)

    def full(b, k, x, dev):
        return remote(pb.at[b, x], fin.at[k, b], nsend.at[k, b], nrecv.at[k, b], dev)

    def step_b(b):
        to_mate(b).wait_recv()
        pb[b] += d2d[b]
        half(b, 0, right).start()
        half(b, 1, left).start()

    def step_c(b):
        half(b, 0, right).wait_recv()
        half(b, 1, left).wait_recv()
        pb[b, rx, 0:H, :] += far[0, b]
        pb[b, lx, H:NT, :] += far[1, b]
        full(b, 0, rx, right).start()
        full(b, 1, lx, left).start()

    def step_d(b, _):
        full(b, 0, rx, right).wait_recv()
        full(b, 1, lx, left).wait_recv()
        out[:, cols(b)] = (acc[:, cols(b)] + pb[b, cx] + fin[0, b] + fin[1, b]).astype(BF)
        return 0

    def combine(b, par, dest):
        for x in range(NX):
            s = x * 2 + par
            place = pl.ds(pl.multiple_of(s * CAP, CAP), CAP)
            r = jnp.concatenate([hr[e, place, FF:FF + BLK] for e in range(NL)], axis=0)
            v = dot(gm[s], r)
            dest[x] = v[0:NT] + (v[NT:2 * NT] + v[2 * NT:3 * NT])

    def second(b, _):
        for p in range(PAIRS):
            q = b * PAIRS + p
            wait(chunk_2(q))
            start_at(SA + SB + Q1 + q - 1 + NS)
            slot = (q + SA + SB + Q1) % NS
            for h in range(2):
                e = 2 * p + h
                hr[e, :, FF:FF + BLK] = dot(hr[e, :, 0:FF], ring[slot, 0:FF, h * BLK:(h + 1) * BLK]).astype(BF)
            if p == 1:
                @pl.when(b >= 1)
                def _():
                    step_b(b - 1)

                @pl.when(b >= 2)
                def _():
                    step_c(b - 2)

        @pl.when(b >= 2)
        def _():
            to_mate(b - 2).wait_send()

        combine(b, 1 - cc, sb.at[b % 2])
        to_mate(b).start()
        combine(b, cc, pb.at[b])
        return 0

    lax.fori_loop(0, NB, second, 0)
    step_b(NB - 1)
    step_c(NB - 2)
    step_c(NB - 1)
    lax.fori_loop(0, NB, step_d, 0)

    for c in metas:
        c.wait_send()
    for c in (x_r0, x_r1, x_l1, x_l0, x_fr, x_fl, p_own, p_l, p_r, p_f0, p_f1, y_r0, y_r1, y_l1, y_l0):
        c.wait_send()
    to_mate(NB - 2).wait_send()
    to_mate(NB - 1).wait_send()

    def drain(b, _):
        half(b, 0, right).wait_send()
        half(b, 1, left).wait_send()
        full(b, 0, rx, right).wait_send()
        full(b, 1, lx, left).wait_send()
        return 0

    lax.fori_loop(0, NB, drain, 0)


def solution(mesh):
    ep_size = mesh.shape["ep"]
    tp_size = mesh.shape["tp"]
    row_spec = P(("data", "ep", "tp"), None)
    expert_spec = P("ep", None, None)

    def layer_body(tokens, expert_ids, gate_vals, slot_ids, send_counts, shared_w1, shared_w3, shared_w2, expert_w1, expert_w3, expert_w2):
        n_tok, d_model = tokens.shape
        top_k = expert_ids.shape[1]
        n_local, _, width = expert_w1.shape
        shared_width = shared_w1.shape[1]
        n_exp = n_local * ep_size
        capacity = capacity_rows(n_tok, top_k, n_exp)
        n_rows = n_exp * capacity

        same = expert_ids[:, :, None] == jnp.arange(n_exp, dtype=jnp.int32)[None, None, :]
        row_limit = jnp.sum(jnp.where(same, send_counts[0][None, None, :], 0), axis=-1)
        kept_mask = (slot_ids >= 0) & (slot_ids < row_limit)
        dest_row = jnp.where(kept_mask, expert_ids * capacity + slot_ids, n_rows).astype(F32)
        gate_eff = jnp.where(kept_mask, gate_vals, 0.0)
        pad = ((0, META // 2 - top_k), (0, 0))
        meta = jnp.concatenate([jnp.pad(dest_row.T, pad), jnp.pad(gate_eff.T, pad)], axis=0)

        ns = 4
        nb = d_model // BLK
        local_rows = n_local * capacity
        cfg = (ep_size, tp_size, n_tok, d_model, width, shared_width, n_local, capacity, top_k, ns)
        half = n_tok // 2
        nx = ep_size // 2
        hbm = pl.BlockSpec(memory_space=pl.ANY)
        vmem = pl.BlockSpec(memory_space=pltpu.VMEM)
        dma = pltpu.SemaphoreType.DMA
        return pl.pallas_call(
            functools.partial(layer_kernel, cfg),
            out_shape=jax.ShapeDtypeStruct((n_tok, d_model), BF),
            in_specs=[hbm, vmem] + [hbm] * 6,
            out_specs=vmem,
            scratch_shapes=[
                pltpu.VMEM((n_local + 1, ep_size * capacity, d_model), BF),
                pltpu.VMEM((ep_size, n_tok, d_model), BF),
                pltpu.VMEM((ep_size, META, n_tok), F32),
                pltpu.VMEM((nb, nx, n_tok, BLK), F32),
                pltpu.VMEM((2, nx, n_tok, BLK), F32),
                pltpu.VMEM((nb, nx, n_tok, BLK), F32),
                pltpu.VMEM((2, nb, half, BLK), F32),
                pltpu.VMEM((2, nb, n_tok, BLK), F32),
                pltpu.VMEM((2, nb, half, BLK), F32),
                pltpu.VMEM((2, nb, n_tok, BLK), F32),
                pltpu.VMEM((n_tok, d_model), F32),
                pltpu.VMEM((tp_size * n_tok, shared_width), BF),
                pltpu.VMEM((2, ep_size * capacity, 2 * BLK), F32),
                pltpu.VMEM((ep_size, 3 * n_tok, local_rows), BF),
                pltpu.VMEM((ns, d_model, 2 * BLK), BF),
                dma, dma((6,)), dma((6,)), dma((5,)), dma((5,)), dma((ep_size - 1,)), dma((ep_size - 1,)),
                dma((6,)), dma((6,)), dma((ns, 2)),
                dma((4,)), dma((4,)), dma((nb,)), dma((nb,)), dma((2, nb)), dma((2, nb)), dma((2, nb)), dma((2, nb)),
            ],
            compiler_params=pltpu.CompilerParams(collective_id=0, has_side_effects=True, vmem_limit_bytes=67043328),
            cost_estimate=pl.CostEstimate(flops=80_000_000_000, bytes_accessed=200_000_000, transcendentals=0),
            name="moe_layer",
        )(tokens, meta, shared_w1, shared_w3, shared_w2, expert_w1, expert_w3, expert_w2)

    return jax.shard_map(
        layer_body,
        mesh=mesh,
        in_specs=(row_spec, row_spec, row_spec, row_spec, row_spec, P(None, "tp"), P(None, "tp"), P("tp", None), expert_spec, expert_spec, expert_spec),
        out_specs=row_spec,
        check_vma=False,
    )
```

time: 613 us -> 168 us (0.27)
  waiting for transfers between devices: 326 us -> 0 us
  Pallas kernels: 0 us -> 163 us
  matrix products: 121 us -> 0 us
  local copies, waits for them, and re-layouts: 112 us -> 1.97 us
  other arithmetic: 25.5 us -> 2.81 us
  starting transfers between devices: 14.4 us -> 0 us
  between operations: 13.6 us -> 0.01 us
    all_to_all x2 -> x0, waiting for transfers between devices: 325 us -> none  [the longest x1 171 us: layer_body(): recv_buf = lax.all_to_all(send_buf, 'ep', 0, 2, tiled=True)]
    pallas_call x0 -> x1, Pallas kernels: none -> 163 us  [layer_body(): pl.pallas_call(functools.partial(layer_kernel, cfg), out_shape=jax.ShapeD...]
    dot_general x4 -> x0, matrix products: 121 us -> none  [the longest x1 62.5 us: layer_body(): jnp.einsum('erf,efd->erd', exp_hidden, expert_w2, preferred_element_type=...]
    gather x6 -> x0, local copies, waits for them, and re-layouts: 44.9 us -> none  [the longest x2 23.1 us: layer_body(): picked = jnp.take(back_rows, dest_row, axis=0, mode='fill', fill_value=0)]
    reshape x3 -> x0, local copies, waits for them, and re-layouts: 32.8 us -> none  [the longest x1 32.5 us: layer_body(): exp_out.reshape(1, n_local, ep_size * capacity, d_model)]
    all_to_all x2 -> x0, local copies, waits for them, and re-layouts: 29.7 us -> none  [the longest x1 16.6 us: layer_body(): lax.all_to_all(exp_out.reshape(1, n_local, ep_size * capacity, d_model),...]
    all_to_all x2 -> x0, starting transfers between devices: 14.4 us -> none  [the longest x1 7.56 us: layer_body(): recv_buf = lax.all_to_all(send_buf, 'ep', 0, 2, tiled=True)]
    select_n x5 -> x0, other arithmetic: 14.2 us -> none  [the longest x1 13.5 us: layer_body(): send_buf = jnp.take(tokens, owner_ids, axis=0, mode='fill', fill_value=0)]
  transfers between devices with their start and end apart: 4 -> 0, of which waited for: 2 -> 0; matrix products, arithmetic and copies ran while one was open for 35% -> 0% of each run, Pallas kernels for 0% -> 0%
where the time goes in v1:
time: 168 us; the launch traced here: 167 us
  Pallas kernels  163 us (97%)
  other arithmetic  2.81 us (2%)
  local copies, waits for them, and re-layouts  1.97 us (1%)
    pallas_call x1, Pallas kernels, layer_body(): pl.pallas_call(functools.partial(layer_kernel, cfg), out_shape=jax.ShapeD...  163 us

profile of v1, /device:TPU:97, one launch (start us, length us, event | category | flops | bytes accessed | tf_op | source)
XLA Modules:
  0.0 167.4 jit_solution(5109638026573217859)
XLA Ops:
  0.0 0.8 select_reduce_fusion
  0.8 0.7 convert_bitcast_fusion
  1.5 0.7 select_bitcast_fusion
  2.2 0.6 select_maximum_fusion.meta
  2.8 162.6 %moe_layer.1 = bf16[128,2560]{1,0:T(8,128)(2,1)} custom-call(bf16[128,2560]{1,0:T(8,128)(2,1)} %tok.1, f32[16,128]{1,0:T(8,128)} %select_maximum_fusion.meta, bf16[2560,768]{1,0:T(8,128)(2,1)} %ws1.1, bf16[2560,768]{1,0:T(8,128)(2,1)} %ws3.1, bf16[768,2560]{1,0:T(8,128)(2,1)} %ws2.1, bf16[8,2560,1536]{2,1,0:T(8,128)(2,1)} %w1.1, bf16[8,2560,1536]{2,1,0:T(8,128)(2,1)} %w3.1, ...), custom_call_target="tpu_custom_call" | custom-call | flops 80000000000 | bytes 200000000 | tf_op jit(solution)/shard_map/moe_layer/pallas_call | solution.py:435
  165.4 2.0 %copy.14 = bf16[128,2560]{1,0:T(8,128)(2,1)} copy(bf16[128,2560]{1,0:T(8,128)(2,1)} %moe_layer.1) | data formatting | bytes 1310720

commit v2 on v1

v2 whole, which is shorter than its diff:
```python
import functools

import jax
import jax.numpy as jnp
from jax import lax
from jax.experimental import pallas as pl
from jax.experimental.pallas import tpu as pltpu
from jax.sharding import PartitionSpec as P

CAP_FACTOR = 4
BF = jnp.bfloat16
F32 = jnp.float32
MESH = pl.DeviceIdType.MESH
BLK = 256
META = 16


def capacity_rows(n_tok, top_k, n_exp):
    return min(n_tok, ((CAP_FACTOR * n_tok * top_k // n_exp + 7) // 8) * 8)


def silu_mul(g, u):
    return (g * (1.0 / (1.0 + jnp.exp(-g))) * u).astype(BF)


def dot(a, b):
    return jnp.dot(a, b, preferred_element_type=F32)


def layer_kernel(cfg, tok, ids, slots, gates, counts, ws1, ws3, ws2, w1, w3, w2, out,
                 hr, xg, yg, mg, pb, sb, d2d, far, fin, yfar, acc, sh, gu, gm, ring,
                 own_sem, xs, xr, ps, pr, ms, mr, ys, yr, wsem,
                 ysend, yrecv, dsend, drecv, fsend, frecv, nsend, nrecv):
    EP, TP, NT, D, FF, FS, NL, CAP, TOPK, NS = cfg
    ROWS = EP * CAP
    LROWS = NL * CAP
    H = NT // 2
    NX = EP // 2
    NB = D // BLK
    C1 = FF // BLK
    Q1 = NL * C1
    PAIRS = NL // 2
    Q2 = NB * PAIRS
    SA = FS // BLK
    SB = D // (2 * BLK)
    K1 = D // BLK
    K2 = FF // BLK
    KG = -(-3 * LROWS // BLK)
    GK = KG * BLK
    KS = FS // BLK
    NE = NL // 2
    G1 = C1 // 3
    G2 = PAIRS // 2
    QE = NE * C1
    PR = 2 * CAP
    O_A = QE
    O_B = O_A + SA
    O_1 = O_B + SB
    O_2 = O_1 + Q1
    total = O_2 + Q2
    ORDER = (0, NX - 1, 1, 2)

    me = lax.axis_index("ep")
    ty = lax.axis_index("tp")
    cx = me // 2
    cc = me % 2
    mate = cx * 2 + (1 - cc)
    rx = (cx + 1) % NX
    lx = (cx + NX - 1) % NX
    right = {"ep": rx * 2 + cc}
    left = {"ep": lx * 2 + cc}
    up = {"tp": (ty + 1) % TP}
    down = {"tp": (ty + TP - 1) % TP}
    partner = {"ep": mate}

    def remote(src, dst, ssem, rsem, dev):
        return pltpu.make_async_remote_copy(src_ref=src, dst_ref=dst, send_sem=ssem, recv_sem=rsem, device_id=dev, device_id_type=MESH)

    def wpair(slot, ra, rb, n):
        return (pltpu.make_async_copy(ra, ring.at[slot, pl.ds(0, n), pl.ds(0, BLK)], wsem.at[slot, 0]),
                pltpu.make_async_copy(rb, ring.at[slot, pl.ds(0, n), pl.ds(BLK, BLK)], wsem.at[slot, 1]))

    def cols(i, w=BLK):
        return pl.ds(pl.multiple_of(i * w, w), w)

    def chunk_w(q, slot):
        e, n = q // C1, q % C1
        return wpair(slot % NS, w1.at[e, :, cols(n)], w3.at[e, :, cols(n)], D)

    def chunk_e(q):
        return chunk_w(q, q)

    def chunk_a(i):
        return wpair((i + O_A) % NS, ws1.at[:, cols(i)], ws3.at[:, cols(i)], D)

    def chunk_b(i):
        return wpair((i + O_B) % NS, ws2.at[:, cols(2 * i)], ws2.at[:, cols(2 * i + 1)], FS)

    def chunk_1(q):
        return chunk_w(q, q + O_1)

    def chunk_2(q):
        b, p = q // PAIRS, q % PAIRS
        return wpair((q + O_2) % NS, w2.at[2 * p, :, cols(b)], w2.at[2 * p + 1, :, cols(b)], FF)

    def start(pair):
        pair[0].start()
        pair[1].start()

    def wait(pair):
        pair[0].wait()
        pair[1].wait()

    def start_at(i):
        bounds = ((0, O_A, chunk_e), (O_A, O_B, chunk_a), (O_B, O_1, chunk_b), (O_1, O_2, chunk_1), (O_2, total, chunk_2))
        for lo, hi, fn in bounds:
            if isinstance(i, int):
                if lo <= i < hi:
                    start(fn(i - lo))
            else:
                @pl.when((i >= lo) & (i < hi))
                def _(fn=fn, lo=lo):
                    start(fn(i - lo))

    own = pltpu.make_async_copy(tok, xg.at[me], own_sem)
    own.start()
    for i in range(NS - 1):
        start_at(i)

    barrier = pltpu.get_barrier_semaphore()
    for d in range(1, EP):
        pl.semaphore_signal(barrier, inc=1, device_id={"ep": (me + d) % EP}, device_id_type=MESH)
    for dev in (up, down):
        pl.semaphore_signal(barrier, inc=1, device_id=dev, device_id_type=MESH)
    own.wait()
    pl.semaphore_wait(barrier, EP + 1)

    lo_h, hi_h, all_h = pl.ds(0, H), pl.ds(H, H), pl.ds(0, NT)

    def xpart(dx, part):
        return xg.at[((cx + dx + NX) % NX) * 2 + cc, part, :]

    def xsend(k, dx, part, dev):
        ref = xpart(dx, part)
        return remote(ref, ref, xs.at[k], xr.at[k], dev)

    x_r0 = xsend(0, 0, lo_h, right)
    x_r1 = xsend(1, 0, hi_h, right)
    x_l1 = xsend(2, 0, hi_h, left)
    x_l0 = xsend(3, 0, lo_h, left)
    x_fr = xsend(4, -1, lo_h, right)
    x_fl = xsend(5, 1, hi_h, left)

    def psend(k, dx, part):
        ref = xpart(dx, part)
        return remote(ref, ref, ps.at[k], pr.at[k], partner)

    p_own = psend(0, 0, all_h)
    p_l = psend(1, -1, all_h)
    p_r = psend(2, 1, all_h)
    p_f0 = psend(3, 2, lo_h)
    p_f1 = psend(4, 2, hi_h)

    def ypart(j, part_start, n):
        return yg.at[pl.ds(j * NT + part_start, n), :]

    y_r0 = remote(xg.at[me, lo_h, :], ypart(0, 0, H), ys.at[0], yr.at[0], up)
    y_r1 = remote(xg.at[me, hi_h, :], ypart(0, H, H), ys.at[1], yr.at[1], up)
    y_l1 = remote(xg.at[me, hi_h, :], ypart(1, H, H), ys.at[2], yr.at[2], down)
    y_l0 = remote(xg.at[me, lo_h, :], ypart(1, 0, H), ys.at[3], yr.at[3], down)
    y_fr = remote(ypart(0, 0, H), ypart(2, 0, H), ys.at[4], yr.at[4], up)
    y_fl = remote(ypart(1, H, H), ypart(2, H, H), ys.at[5], yr.at[5], down)

    metas = [remote(mg.at[me], mg.at[me], ms.at[d - 1], mr.at[d - 1], {"ep": (me + d) % EP}) for d in range(1, EP)]

    d_mate = (me + EP - mate) % EP
    mate_meta = remote(mg.at[mate], mg.at[mate], ms.at[d_mate - 1], mr.at[d_mate - 1], partner)

    for c in (x_r0, x_l1, y_r0, y_l1, p_own, x_r1, x_l0, y_r1, y_l0):
        c.start()
    mg[me] = jnp.zeros((META, NT), F32)

    id_t = ids[...].astype(F32)
    slot_t = slots[...].astype(F32)
    limit = jnp.zeros_like(id_t)
    for e in range(NL * EP):
        limit = jnp.where(id_t == float(e), counts[0, e].astype(F32), limit)
    kept = (slot_t >= 0.0) & (slot_t < limit)
    mg[me, 0:TOPK, :] = jnp.where(kept, id_t * float(CAP) + slot_t, float(NL * EP * CAP))
    mg[me, 8:8 + TOPK, :] = jnp.where(kept, gates[...], 0.0)
    for c in metas:
        c.start()

    row_id = lax.broadcasted_iota(jnp.int32, (LROWS, NT), 0).astype(F32) + (me * LROWS).astype(F32)

    def gather(j, _):
        dx = (3 * j + 3 * (j // 2) - 2 * (j // 3)) % NX
        x0 = ((cx + dx) % NX) * 2
        for c in range(2):
            m = mg[x0 + c]
            pick = jnp.zeros((LROWS, NT), F32)
            wgt = jnp.zeros((LROWS, NT), F32)
            for t in range(TOPK):
                hit = m[t:t + 1, :] == row_id
                pick = jnp.where(hit, 1.0, pick)
                wgt = wgt + jnp.where(hit, m[8 + t:9 + t, :], 0.0)
            pick = pick.astype(BF)
            wt = jnp.transpose(wgt)
            hi = wt.astype(BF)
            rest = wt - hi.astype(F32)
            mid = rest.astype(BF)
            low = (rest - mid.astype(F32)).astype(BF)
            gm[x0 + c, :, 0:LROWS] = hi
            gm[x0 + c, :, LROWS:2 * LROWS] = mid
            gm[x0 + c, :, 2 * LROWS:3 * LROWS] = low
            if GK > 3 * LROWS:
                gm[x0 + c, :, 3 * LROWS:GK] = jnp.zeros((NT, GK - 3 * LROWS), BF)
            place = pl.ds(pl.multiple_of(j * PR + c * CAP, 16), CAP)
            for n in range(D // 512):
                part = slice(n * 512, (n + 1) * 512)
                got = dot(pick, xg[x0 + c, :, part]).astype(BF)
                for e in range(NL):
                    hr[e + 1, place, part] = got[e * CAP:(e + 1) * CAP, :]
        return 0

    def early(e, _):
        @pl.when(e == NE // 2)
        def _():
            relay()

        @pl.when(e == NE - 1)
        def _():
            x_r1.wait_recv()
            p_l.start()
            x_l0.wait_recv()
            p_r.start()

        for n in range(C1):
            q = e * C1 + n
            wait(chunk_e(q))
            start_at(q - 1 + NS)
            r = dot(hr[e + 1, 0:PR, :], ring[q % NS])
            hr[e, 0:PR, n * BLK:(n + 1) * BLK] = silu_mul(r[:, :BLK], r[:, BLK:])
        return 0

    def relay():
        x_r0.wait_recv()
        x_fr.start()
        x_l1.wait_recv()
        x_fl.start()
        y_r0.wait_recv()
        y_fr.start()
        y_l1.wait_recv()
        y_fl.start()

    def shared():
        def stretch(lo, hi, free):
            for i in range(lo, hi):
                wait(chunk_a(i - O_A) if i < O_B else chunk_b(i - O_B))
            for i in range(free, lo):
                start_at(i + NS)
            for i in range(lo, hi):
                if i < O_B:
                    here = slice((i - O_A) * BLK, (i - O_A + 1) * BLK)
                    r = dot(yg[...], ring[i % NS])
                    sh[NT:, here] = silu_mul(r[:, :BLK], r[:, BLK:])
                    r = dot(xg[me], ring[i % NS])
                    sh[0:NT, here] = silu_mul(r[:, :BLK], r[:, BLK:])
                else:
                    b = i - O_B
                    r = dot(sh[...], ring[i % NS, 0:FS, :])
                    here = slice(2 * b * BLK, (2 * b + 2) * BLK)
                    acc[:, here] = xg[me, :, here].astype(F32) + r[0:NT]
                    for j in range(3):
                        for m in range(2):
                            pb[2 * b + m, j] = r[(j + 1) * NT:(j + 2) * NT, m * BLK:(m + 1) * BLK]

        stretch(O_A, O_B, O_A - 1)
        stretch(O_B, O_B + 3, O_A)
        stretch(O_B + 3, O_1, O_B)

    def head():
        mate_meta.wait_recv()
        p_own.wait_recv()
        lax.fori_loop(0, 1, gather, 0)
        lax.fori_loop(0, NE, early, 0)
        for d in range(1, EP):
            @pl.when(d != d_mate)
            def _(d=d):
                metas[d - 1].wait_recv()

        y_r1.wait_recv()
        y_l0.wait_recv()
        p_l.wait_recv()
        p_r.wait_recv()
        lax.fori_loop(1, NX - 1, gather, 0)
        x_fr.wait_recv()
        p_f0.start()
        x_fl.wait_recv()
        p_f1.start()
        y_fr.wait_recv()
        y_fl.wait_recv()
        shared()
        for c in y_halves:
            c.start()
        p_f0.wait_recv()
        p_f1.wait_recv()
        lax.fori_loop(NX - 1, NX, gather, 0)

    def y_half(k, dev):
        return remote(pb.at[:, 2, pl.ds(k * H, H), :], yfar.at[k], ysend.at[k], yrecv.at[k], dev)

    def y_full(k, j, dev):
        return remote(pb.at[:, j], fin.at[k], ysend.at[2 + k], yrecv.at[2 + k], dev)

    y_halves = (y_half(0, up), y_half(1, down))
    y_fulls = (y_full(0, 1, up), y_full(1, 0, down))
    def y_step2():
        for c in y_halves:
            c.wait()

        def add(i, _):
            pb[i, 1, 0:H, :] += yfar[0, i]
            pb[i, 0, H:NT, :] += yfar[1, i]
            return 0

        lax.fori_loop(0, NB, add, 0)
        for c in y_fulls:
            c.start()

    def y_step3():
        for c in y_fulls:
            c.wait()

        def add(i, _):
            acc[:, cols(i)] += fin[0, i] + fin[1, i]
            return 0

        lax.fori_loop(0, NB, add, 0)

    def finish(r, r0, e, n):
        hr[e, r0:ROWS, n * BLK:(n + 1) * BLK] = silu_mul(r[:, :BLK], r[:, BLK:])

    def first(r0, e0, e, _):
        if e0 == 0:
            @pl.when(e == NE - 1)
            def _():
                y_step2()

        for h in range(C1 // G1):
            q = e * C1 + h * G1
            for i in range(G1):
                wait(chunk_1(q + i))
            for i in range(G1):
                ahead = q + NS - G1 + i
                past = (h - 1) * G1 + NS + i - C1
                if e0 == 0 or past < 0:
                    start(chunk_1(ahead))
                else:
                    @pl.when(ahead < Q1)
                    def _(ahead=ahead):
                        start(chunk_1(ahead))

                    @pl.when(ahead >= Q1)
                    def _(past=past):
                        start(chunk_2(past))
            rows = hr[e + 1, r0:ROWS, :]
            for i in range(G1):
                n = h * G1 + i
                r = dot(rows, ring[(O_1 + n) % NS])
                if i == 0:
                    if h:
                        finish(gu[r0:ROWS], r0, e, n - 1)
                    else:
                        finish(gu[r0:ROWS], r0, jnp.maximum(e - 1, e0), C1 - 1)
                if i + 1 < G1:
                    finish(r, r0, e, n)
                else:
                    gu[r0:ROWS] = r
        return 0

    def middle():
        lax.fori_loop(0, NE, functools.partial(first, PR, 0), 0)
        finish(gu[PR:ROWS], PR, NE - 1, C1 - 1)
        lax.fori_loop(NE, NL, functools.partial(first, 0, NE), 0)
        finish(gu[...], 0, NL - 1, C1 - 1)
        y_step3()

    def to_mate(b):
        return remote(sb.at[b % 2], d2d.at[b % 2], dsend.at[b], drecv.at[b], partner)

    def half(b, k, dev):
        return remote(pb.at[b, 3, pl.ds(k * H, H), :], far.at[k, b], fsend.at[k, b], frecv.at[k, b], dev)

    def full(b, k, dev):
        return remote(pb.at[b, 2 - k], fin.at[k, b], nsend.at[k, b], nrecv.at[k, b], dev)

    def step_b(b):
        to_mate(b).wait_recv()
        pb[b] += d2d[b % 2]
        half(b, 0, right).start()
        half(b, 1, left).start()

    def step_c(b):
        half(b, 0, right).wait_recv()
        half(b, 1, left).wait_recv()
        pb[b, 2, 0:H, :] += far[0, b]
        pb[b, 1, H:NT, :] += far[1, b]
        full(b, 0, right).start()
        full(b, 1, left).start()

    def step_d(b, _):
        full(b, 0, right).wait_recv()
        full(b, 1, left).wait_recv()
        out[:, cols(b)] = (acc[:, cols(b)] + pb[b, 0] + fin[0, b] + fin[1, b]).astype(BF)
        return 0

    side = slice(FF, FF + BLK)

    def combine(b):
        half_x = NX // 2
        for i in range(2):
            par = (1 - cc, cc)[i]
            for j in range(NX):
                src = ((cx + ORDER[j]) % NX) * 2 + par
                place = pl.ds(pl.multiple_of((2 * j + par) * CAP, 16), CAP)
                r = [hr[e, place, side] for e in range(NL)] * 3
                if GK > 3 * LROWS:
                    r.append(jnp.zeros((GK - 3 * LROWS, BLK), BF))
                v = dot(gm[src], jnp.concatenate(r, axis=0))
                if i == 0:
                    sb[b % 2, j] = v
                else:
                    pb[b, j] = v

    def pairs(b, h):
        q = b * PAIRS + h * G2
        for i in range(G2):
            wait(chunk_2(q + i))
        for i in range(G2):
            @pl.when(q + NS - G2 + i < Q2)
            def _(i=i):
                start(chunk_2(q + NS - G2 + i))

    def rows_out(b, h):
        q = b * PAIRS + h * G2
        for i in range(G2):
            slot = (q + O_2 + i) % NS
            for m in range(2):
                e = 2 * (h * G2 + i) + m
                hr[e, :, side] = dot(hr[e, :, 0:FF], ring[slot, 0:FF, m * BLK:(m + 1) * BLK]).astype(BF)

    def second(b, _):
        pairs(b, 0)
        rows_out(b, 0)

        @pl.when(b >= 1)
        def _():
            step_b(b - 1)

        @pl.when(b >= 2)
        def _():
            step_c(b - 2)
            to_mate(b - 2).wait_send()

        @pl.when(b >= 5)
        def _():
            step_d(b - 5, 0)

        pairs(b, 1)
        rows_out(b, 1)
        combine(b)
        to_mate(b).start()
        return 0

    head()
    middle()
    lax.fori_loop(0, NB, second, 0)
    step_b(NB - 1)
    step_c(NB - 2)
    step_c(NB - 1)
    lax.fori_loop(NB - 5, NB, step_d, 0)

    for c in metas:
        c.wait_send()
    for c in (x_r0, x_r1, x_l1, x_l0, x_fr, x_fl, p_own, p_l, p_r, p_f0, p_f1, y_r0, y_r1, y_l1, y_l0, y_fr, y_fl):
        c.wait_send()
    to_mate(NB - 2).wait_send()
    to_mate(NB - 1).wait_send()

    def drain(b, _):
        half(b, 0, right).wait_send()
        half(b, 1, left).wait_send()
        full(b, 0, right).wait_send()
        full(b, 1, left).wait_send()
        return 0

    lax.fori_loop(0, NB, drain, 0)


def solution(mesh):
    ep_size = mesh.shape["ep"]
    tp_size = mesh.shape["tp"]
    row_spec = P(("data", "ep", "tp"), None)
    expert_spec = P("ep", None, None)

    def layer_body(tokens, expert_ids, gate_vals, slot_ids, send_counts, shared_w1, shared_w3, shared_w2, expert_w1, expert_w3, expert_w2):
        n_tok, d_model = tokens.shape
        top_k = expert_ids.shape[1]
        n_local, _, width = expert_w1.shape
        shared_width = shared_w1.shape[1]
        n_exp = n_local * ep_size
        capacity = capacity_rows(n_tok, top_k, n_exp)
        ns = 6
        nb = d_model // BLK
        local_rows = n_local * capacity
        cfg = (ep_size, tp_size, n_tok, d_model, width, shared_width, n_local, capacity, top_k, ns)
        half = n_tok // 2
        nx = ep_size // 2
        hbm = pl.BlockSpec(memory_space=pl.ANY)
        vmem = pl.BlockSpec(memory_space=pltpu.VMEM)
        dma = pltpu.SemaphoreType.DMA
        return pl.pallas_call(
            functools.partial(layer_kernel, cfg),
            out_shape=jax.ShapeDtypeStruct((n_tok, d_model), BF),
            in_specs=[hbm, vmem, vmem, vmem, pl.BlockSpec(memory_space=pltpu.SMEM)] + [hbm] * 6,
            out_specs=vmem,
            scratch_shapes=[
                pltpu.VMEM((n_local + 1, ep_size * capacity, d_model), BF),
                pltpu.VMEM((ep_size, n_tok, d_model), BF),
                pltpu.VMEM(((tp_size - 1) * n_tok, d_model), BF),
                pltpu.VMEM((ep_size, META, n_tok), F32),
                pltpu.VMEM((nb, nx, n_tok, BLK), F32),
                pltpu.VMEM((2, nx, n_tok, BLK), F32),
                pltpu.VMEM((2, nx, n_tok, BLK), F32),
                pltpu.VMEM((2, nb, half, BLK), F32),
                pltpu.VMEM((2, nb, n_tok, BLK), F32),
                pltpu.VMEM((2, nb, half, BLK), F32),
                pltpu.VMEM((n_tok, d_model), F32),
                pltpu.VMEM((tp_size * n_tok, shared_width), BF),
                pltpu.VMEM((ep_size * capacity, 2 * BLK), F32),
                                pltpu.VMEM((ep_size, n_tok, -(-3 * local_rows // BLK) * BLK), BF),
                pltpu.VMEM((ns, d_model, 2 * BLK), BF),
                dma, dma((6,)), dma((6,)), dma((5,)), dma((5,)), dma((ep_size - 1,)), dma((ep_size - 1,)),
                dma((6,)), dma((6,)), dma((ns, 2)),
                dma((4,)), dma((4,)), dma((nb,)), dma((nb,)), dma((2, nb)), dma((2, nb)), dma((2, nb)), dma((2, nb)),
            ],
            compiler_params=pltpu.CompilerParams(collective_id=0, has_side_effects=True, vmem_limit_bytes=67043328),
            cost_estimate=pl.CostEstimate(flops=80_000_000_000, bytes_accessed=200_000_000, transcendentals=0),
            name="moe_layer",
        )(tokens, expert_ids.T, slot_ids.T, gate_vals.T, send_counts, shared_w1, shared_w3, shared_w2, expert_w1, expert_w3, expert_w2)

    return jax.shard_map(
        layer_body,
        mesh=mesh,
        in_specs=(row_spec, row_spec, row_spec, row_spec, row_spec, P(None, "tp"), P(None, "tp"), P("tp", None), expert_spec, expert_spec, expert_spec),
        out_specs=row_spec,
        check_vma=False,
    )
```

time: 168 us -> 148 us (0.88)
  Pallas kernels: 163 us -> 146 us
  other arithmetic: 2.81 us -> 0 us
    pallas_call x1, Pallas kernels: 163 us -> 146 us  [layer_body(): pl.pallas_call(functools.partial(layer_kernel, cfg), out_shape=jax.ShapeD...]
where the time goes in v2:
time: 148 us
  Pallas kernels  146 us (99%)
  local copies, waits for them, and re-layouts  1.97 us (1%)
    pallas_call x1, Pallas kernels, layer_body(): pl.pallas_call(functools.partial(layer_kernel, cfg), out_shape=jax.ShapeD...  146 us

profile of v2, /device:TPU:97, one launch (start us, length us, event | category | flops | bytes accessed | tf_op | source)
XLA Modules:
  0.0 148.3 jit_solution(18348815406187869257)
XLA Ops:
  0.0 146.3 %moe_layer.1 = bf16[128,2560]{1,0:T(8,128)(2,1)} custom-call(bf16[128,2560]{1,0:T(8,128)(2,1)} %tok.1, s32[6,128]{1,0:T(8,128)} %bitcast.3, s32[6,128]{1,0:T(8,128)} %bitcast.4, f32[6,128]{1,0:T(8,128)} %bitcast.5, s32[1,64]{1,0:T(1,128)} %counts.1, bf16[2560,768]{1,0:T(8,128)(2,1)} %ws1.1, bf16[2560,768]{1,0:T(8,128)(2,1)} %ws3.1, bf16[768,2560]{1,0:T(8,128)(2,1)} %ws2.1, ...), custom_call_target="tpu_custom_call" | custom-call | flops 80000000000 | bytes 200000000 | tf_op jit(solution)/shard_map/moe_layer/pallas_call | solution.py:523
  146.3 2.0 %copy.13 = bf16[128,2560]{1,0:T(8,128)(2,1)} copy(bf16[128,2560]{1,0:T(8,128)(2,1)} %moe_layer.1) | data formatting | bytes 1310720

commit v3 on v2

--- a/solution.py
+++ b/solution.py
@@ -28,7 +28,7 @@
 
 
 def layer_kernel(cfg, tok, ids, slots, gates, counts, ws1, ws3, ws2, w1, w3, w2, out,
-                 hr, xg, yg, mg, pb, sb, d2d, far, fin, yfar, acc, sh, gu, gm, ring,
+                 hr, xg, yg, mg, pb, sb, d2d, far, fin, yfar, yfin, acc, sh, gu, gm, ring,
                  own_sem, xs, xr, ps, pr, ms, mr, ys, yr, wsem,
                  ysend, yrecv, dsend, drecv, fsend, frecv, nsend, nrecv):
     EP, TP, NT, D, FF, FS, NL, CAP, TOPK, NS = cfg
@@ -124,8 +124,6 @@
 
     own = pltpu.make_async_copy(tok, xg.at[me], own_sem)
     own.start()
-    for i in range(NS - 1):
-        start_at(i)
 
     barrier = pltpu.get_barrier_semaphore()
     for d in range(1, EP):
@@ -133,6 +131,8 @@
     for dev in (up, down):
         pl.semaphore_signal(barrier, inc=1, device_id=dev, device_id_type=MESH)
     own.wait()
+    for i in range(NS - 1):
+        start_at(i)
     pl.semaphore_wait(barrier, EP + 1)
 
     lo_h, hi_h, all_h = pl.ds(0, H), pl.ds(H, H), pl.ds(0, NT)
@@ -301,7 +301,7 @@
         y_fr.wait_recv()
         y_fl.wait_recv()
         shared()
-        for c in y_halves:
+        for c in y_halves + y_plain:
             c.start()
         p_f0.wait_recv()
         p_f1.wait_recv()
@@ -310,11 +310,13 @@
     def y_half(k, dev):
         return remote(pb.at[:, 2, pl.ds(k * H, H), :], yfar.at[k], ysend.at[k], yrecv.at[k], dev)
 
-    def y_full(k, j, dev):
-        return remote(pb.at[:, j], fin.at[k], ysend.at[2 + k], yrecv.at[2 + k], dev)
+    def y_part(i, j, part, dev):
+        return remote(pb.at[:, j, part, :], yfin.at[1 - j, :, part, :], ysend.at[2 + i], yrecv.at[2 + i], dev)
 
     y_halves = (y_half(0, up), y_half(1, down))
-    y_fulls = (y_full(0, 1, up), y_full(1, 0, down))
+    y_plain = (y_part(0, 1, hi_h, up), y_part(1, 0, lo_h, down))
+    y_added = (y_part(2, 1, lo_h, up), y_part(3, 0, hi_h, down))
+
     def y_step2():
         for c in y_halves:
             c.wait()
@@ -325,15 +327,15 @@
             return 0
 
         lax.fori_loop(0, NB, add, 0)
-        for c in y_fulls:
+        for c in y_added:
             c.start()
 
     def y_step3():
-        for c in y_fulls:
+        for c in y_plain + y_added:
             c.wait()
 
         def add(i, _):
-            acc[:, cols(i)] += fin[0, i] + fin[1, i]
+            acc[:, cols(i)] += yfin[0, i] + yfin[1, i]
             return 0
 
         lax.fori_loop(0, NB, add, 0)
@@ -342,8 +344,8 @@
         hr[e, r0:ROWS, n * BLK:(n + 1) * BLK] = silu_mul(r[:, :BLK], r[:, BLK:])
 
     def first(r0, e0, e, _):
-        if e0 == 0:
-            @pl.when(e == NE - 1)
+        if e0:
+            @pl.when(e == e0)
             def _():
                 y_step2()
 
@@ -387,31 +389,59 @@
         y_step3()
 
     def to_mate(b):
-        return remote(sb.at[b % 2], d2d.at[b % 2], dsend.at[b], drecv.at[b], partner)
+        return remote(sb.at[b % 2], d2d.at[b % 2], dsend.at[b % 2], drecv.at[b], partner)
 
     def half(b, k, dev):
-        return remote(pb.at[b, 3, pl.ds(k * H, H), :], far.at[k, b], fsend.at[k, b], frecv.at[k, b], dev)
-
-    def full(b, k, dev):
-        return remote(pb.at[b, 2 - k], fin.at[k, b], nsend.at[k, b], nrecv.at[k, b], dev)
+        return remote(pb.at[b, 3, pl.ds(k * H, H), :], far.at[k, b], fsend.at[k, b % 2], frecv.at[k, b], dev)
+
+    def part(b, i, dev):
+        k = i % 2
+        rows = (hi_h, lo_h, lo_h, hi_h)[i]
+        return remote(pb.at[b, 2 - k, rows, :], fin.at[k, b, rows, :], nsend.at[i, b % 2], nrecv.at[i, b], dev)
+
+    sides = (right, left, right, left)
+
+    def sent_b(b):
+        half(b, 0, right).wait_send()
+        half(b, 1, left).wait_send()
+        for i in (0, 1):
+            part(b, i, sides[i]).wait_send()
+
+    def sent_c(b):
+        for i in (2, 3):
+            part(b, i, sides[i]).wait_send()
 
     def step_b(b):
         to_mate(b).wait_recv()
         pb[b] += d2d[b % 2]
+        if isinstance(b, int):
+            sent_b(b - 2)
+        else:
+            @pl.when(b >= 2)
+            def _():
+                sent_b(b - 2)
         half(b, 0, right).start()
         half(b, 1, left).start()
+        for i in (0, 1):
+            part(b, i, sides[i]).start()
 
     def step_c(b):
         half(b, 0, right).wait_recv()
         half(b, 1, left).wait_recv()
         pb[b, 2, 0:H, :] += far[0, b]
         pb[b, 1, H:NT, :] += far[1, b]
-        full(b, 0, right).start()
-        full(b, 1, left).start()
+        if isinstance(b, int):
+            sent_c(b - 2)
+        else:
+            @pl.when(b >= 2)
+            def _():
+                sent_c(b - 2)
+        for i in (2, 3):
+            part(b, i, sides[i]).start()
 
     def step_d(b, _):
-        full(b, 0, right).wait_recv()
-        full(b, 1, left).wait_recv()
+        for i in range(4):
+            part(b, i, sides[i]).wait_recv()
         out[:, cols(b)] = (acc[:, cols(b)] + pb[b, 0] + fin[0, b] + fin[1, b]).astype(BF)
         return 0
 
@@ -432,6 +462,8 @@
                     sb[b % 2, j] = v
                 else:
                     pb[b, j] = v
+            if i == 0:
+                to_mate(b).start()
 
     def pairs(b, h):
         q = b * PAIRS + h * G2
@@ -470,7 +502,6 @@
         pairs(b, 1)
         rows_out(b, 1)
         combine(b)
-        to_mate(b).start()
         return 0
 
     head()
@@ -488,14 +519,9 @@
     to_mate(NB - 2).wait_send()
     to_mate(NB - 1).wait_send()
 
-    def drain(b, _):
-        half(b, 0, right).wait_send()
-        half(b, 1, left).wait_send()
-        full(b, 0, right).wait_send()
-        full(b, 1, left).wait_send()
-        return 0
-
-    lax.fori_loop(0, NB, drain, 0)
+    for b in (NB - 2, NB - 1):
+        sent_b(b)
+        sent_c(b)
 
 
 def solution(mesh):
@@ -536,6 +562,7 @@
                 pltpu.VMEM((2, nb, half, BLK), F32),
                 pltpu.VMEM((2, nb, n_tok, BLK), F32),
                 pltpu.VMEM((2, nb, half, BLK), F32),
+                pltpu.VMEM((2, nb, n_tok, BLK), F32),
                 pltpu.VMEM((n_tok, d_model), F32),
                 pltpu.VMEM((tp_size * n_tok, shared_width), BF),
                 pltpu.VMEM((ep_size * capacity, 2 * BLK), F32),
@@ -543,7 +570,7 @@
                 pltpu.VMEM((ns, d_model, 2 * BLK), BF),
                 dma, dma((6,)), dma((6,)), dma((5,)), dma((5,)), dma((ep_size - 1,)), dma((ep_size - 1,)),
                 dma((6,)), dma((6,)), dma((ns, 2)),
-                dma((4,)), dma((4,)), dma((nb,)), dma((nb,)), dma((2, nb)), dma((2, nb)), dma((2, nb)), dma((2, nb)),
+                dma((6,)), dma((6,)), dma((2,)), dma((nb,)), dma((2, 2)), dma((2, nb)), dma((4, 2)), dma((4, nb)),
             ],
             compiler_params=pltpu.CompilerParams(collective_id=0, has_side_effects=True, vmem_limit_bytes=67043328),
             cost_estimate=pl.CostEstimate(flops=80_000_000_000, bytes_accessed=200_000_000, transcendentals=0),

time: 148 us -> 144 us (0.973)
  Pallas kernels: 146 us -> 142 us
    pallas_call x1, Pallas kernels: 146 us -> 142 us  [layer_body(): pl.pallas_call(functools.partial(layer_kernel, cfg), out_shape=jax.ShapeD...]
where the time goes in v3:
time: 144 us
  Pallas kernels  142 us (99%)
  local copies, waits for them, and re-layouts  1.97 us (1%)
    pallas_call x1, Pallas kernels, layer_body(): pl.pallas_call(functools.partial(layer_kernel, cfg), out_shape=jax.ShapeD...  142 us

profile of v3, /device:TPU:97, one launch (start us, length us, event | category | flops | bytes accessed | tf_op | source)
XLA Modules:
  0.0 144.0 jit_solution(13814903372274991173)
XLA Ops:
  0.0 142.0 %moe_layer.1 = bf16[128,2560]{1,0:T(8,128)(2,1)} custom-call(bf16[128,2560]{1,0:T(8,128)(2,1)} %tok.1, s32[6,128]{1,0:T(8,128)} %bitcast.3, s32[6,128]{1,0:T(8,128)} %bitcast.4, f32[6,128]{1,0:T(8,128)} %bitcast.5, s32[1,64]{1,0:T(1,128)} %counts.1, bf16[2560,768]{1,0:T(8,128)(2,1)} %ws1.1, bf16[2560,768]{1,0:T(8,128)(2,1)} %ws3.1, bf16[768,2560]{1,0:T(8,128)(2,1)} %ws2.1, ...), custom_call_target="tpu_custom_call" | custom-call | flops 80000000000 | bytes 200000000 | tf_op jit(solution)/shard_map/moe_layer/pallas_call | solution.py:549
  142.0 2.0 %copy.13 = bf16[128,2560]{1,0:T(8,128)(2,1)} copy(bf16[128,2560]{1,0:T(8,128)(2,1)} %moe_layer.1) | data formatting | bytes 1310720
